TPU v7x, 512 devices: a whole 4x4x16 slice. The times are simulated.
512 devices in a mesh: grp: 64 (over z, x_lo, core), tp: 8 (over x_hi, y).
Axes of the slice: x: 4 (x_hi: 2, x_lo: 2; x = x_hi * 2 + x_lo), y: 4, z: 16, core: 2. Of those that a mesh axis runs over, the one named last changes fastest.
Arguments:
- memory_rows: bfloat16 [65536, 4096], P('grp', 'tp'), may hold values from -24 to 24, as said below
- norm_gain: float32 [4096], replicated, may hold values from 0.25 to 1.75
- key_weight: bfloat16 [4096, 4096], P(None, 'tp'), may hold values from -0.09375 to 0.09375
- owner_table: int32 [8192], replicated, may hold values from 0 to 8191, as said below
Outputs:
- placed_keys: bfloat16 [65536, 4096], P('grp', 'tp')
Inputs may be any that keep to these rules, and one draw needn't show every extreme that they name: A permutation of the 8192 block numbers. Block b of the input goes to block position owner_table[b], which lies in group owner_table[b] // 128. The 128 blocks of one group go to all 64 groups, exactly 2 blocks to each of them. `memory_rows`: rows have offsets and scales of their own, and features a common pattern.
All inputs are finite; a program needn't handle non-finite values.
Results may differ from a plain program's by a relative error of at most 0.0049.
Values may be sent and summed in bfloat16 or wider, within the bound.
No kernel may reach another device: no remote copies, remote signals or barrier semaphores. Data moves between devices by JAX's collectives and lax.ppermute only.
A program may use at most 64 MiB of HBM per device.

v0:
```python
import jax
import jax.numpy as jnp
from jax import lax
from jax.sharding import PartitionSpec as P

BLK_ROWS = 8
EPS = 1e-05


def to_owners(block_rows, owner_table):
    groups = lax.axis_size("grp")
    position = lax.axis_index("grp")
    row_count, col_count = block_rows.shape
    blocks_here = row_count // BLK_ROWS
    capacity = max(1, blocks_here // groups)
    owned_slots = lax.dynamic_slice_in_dim(owner_table, position * blocks_here, blocks_here)
    target = owned_slots // blocks_here
    block_ids = jnp.arange(blocks_here, dtype=jnp.int32)
    earlier = (target[None, :] == target[:, None]) & (block_ids[None, :] < block_ids[:, None])
    rank = jnp.sum(earlier.astype(jnp.int32), axis=1)
    send_slot = target * capacity + rank
    slot_ids = jnp.arange(groups * capacity, dtype=jnp.int32)
    sender = (send_slot[None, :] == slot_ids[:, None]).astype(jnp.bfloat16)
    flattened = block_rows.reshape(blocks_here, BLK_ROWS * col_count)
    outgoing = jnp.dot(sender, flattened, preferred_element_type=jnp.float32).astype(jnp.bfloat16)
    incoming = lax.all_to_all(outgoing, "grp", split_axis=0, concat_axis=0, tiled=True)
    block_total = owner_table.shape[0]
    inverse = (
        jnp.zeros((block_total,), jnp.int32)
        .at[owner_table]
        .set(jnp.arange(block_total, dtype=jnp.int32))
    )
    arriving = lax.dynamic_slice_in_dim(inverse, position * blocks_here, blocks_here)
    anchor_group = arriving // blocks_here
    anchor_column = arriving % blocks_here
    target_table = owner_table.reshape(groups, blocks_here) // blocks_here
    anchor_targets = target_table[anchor_group]
    before = (anchor_targets == position) & (block_ids[None, :] < anchor_column[:, None])
    anchor_rank = jnp.sum(before.astype(jnp.int32), axis=1)
    source_slot = anchor_group * capacity + anchor_rank
    picker = (source_slot[:, None] == slot_ids[None, :]).astype(jnp.bfloat16)
    placed = jnp.dot(picker, incoming, preferred_element_type=jnp.float32).astype(jnp.bfloat16)
    return placed.reshape(row_count, col_count)


def project(memory_rows, norm_gain, key_weight):
    width = norm_gain.shape[0]
    whole_rows = lax.all_gather(memory_rows, "tp", axis=1, tiled=True)
    values = whole_rows.astype(jnp.float32)
    row_mean = jnp.sum(values, axis=1, keepdims=True) / width
    row_var = jnp.sum(values * values, axis=1, keepdims=True) / width - row_mean * row_mean
    normed = ((values - row_mean) * lax.rsqrt(row_var + EPS) * norm_gain[None, :]).astype(
        jnp.bfloat16
    )
    keys = jnp.dot(normed, key_weight, preferred_element_type=jnp.float32)
    return keys.astype(jnp.bfloat16)


def on_device(memory_rows, norm_gain, key_weight, owner_table):
    keys = project(memory_rows, norm_gain, key_weight)
    return to_owners(keys, owner_table)


def solution(mesh):
    in_specs = (P("grp", "tp"), P(), P(None, "tp"), P())
    out_specs = P("grp", "tp")
    return jax.shard_map(
        on_device, mesh=mesh, in_specs=in_specs, out_specs=out_specs, check_vma=False
    )
```

profile of v0, /device:TPU:2, one launch (start us, length us, event | category | flops | bytes accessed | tf_op | source)
XLA Modules:
  0.0 236.6 jit_solution(608830909230115830)
XLA Ops:
  6.5 0.0 copy-start.2
  6.5 0.0 all-gather.2.cloned.1.call-start
  6.5 0.7 all-gather.2.cloned.1.call-update
  7.3 0.8 and_select_fusion
  8.0 0.2 convert_reduce_fusion.1
  8.2 0.8 multiply_add_fusion
  9.0 132.8 %all-gather.2.cloned.1.call-done = bf16[1024,4096]{1,0:T(8,128)(2,1)} async-done(((bf16[1024,512]{1,0:T(8,128)(2,1)}), bf16[1024,4096]{1,0:T(8,128)(2,1)}) %all-gather.2.cloned.1.call-update) | async-done | bytes 8388624 | tf_op jit(solution)/shard_map/all_gather | solution.py:48
  141.8 0.0 copy-start
  141.8 6.1 %convert_reduce_fusion = (f32[1024]{0:T(1024)S(1)}, f32[1024]{0:T(1024)S(1)}) fusion(bf16[1024,4096]{1,0:T(8,128)(2,1)} %all-gather.2.cloned.1.call-done), kind=kLoop, calls=%fused_computation.4 | loop fusion | flops 16775168 | bytes 8396800 | tf_op jit(solution)/shard_map/reduce_sum | solution.py:50
  147.9 0.0 copy-done.2
  147.9 0.0 copy-done
  147.9 6.8 %fusion.9 = bf16[1024,512]{1,0:T(8,128)(2,1)S(1)} fusion(bf16[4096,512]{1,0:T(8,128)(2,1)} %param.6, bf16[1024,4096]{1,0:T(8,128)(2,1)S(1)} %copy-done, f32[4096]{0:T(1024)S(1)} %copy-done.2, f32[1024]{0:T(1024)S(1)} %get-tuple-element.12, f32[1024]{0:T(1024)S(1)} %get-tuple-element.11), kind=kOutput, calls=%fused_computation.15 | convolution fusion | flops 4316463104 | bytes 13656064 | tf_op jit(solution)/shard_map/dot_general | solution.py:55
  154.8 0.0 copy-start.1
  154.8 0.5 reshape.36
  155.3 0.4 convolution_convert_fusion.1
  155.8 1.5 all_to_all.8
  157.3 14.2 %all-to-all-start = ((bf16[64,2,4096]{2,1,0:T(2,128)(2,1)}), bf16[64,2,4096]{2,1,0:T(2,128)(2,1)S(1)}, u32[]{:S(2)}, u32[]{:S(2)}) async-start(bf16[64,2,4096]{2,1,0:T(2,128)(2,1)} %all_to_all.8), calls=%async_computation | async-start | bytes 2097152 | tf_op jit(solution)/shard_map/all_to_all | solution.py:26
  171.5 0.0 copy-done.1
  171.5 30.5 %scatter_custom_fusion = s32[8192]{0:T(1024)S(1)} fusion(s32[8192]{0:T(1024)S(1)} %compare_select_fusion, s32[8192]{0:T(1024)S(1)} %iota.11, s32[]{:T(128)} %constant.54.clone.1), kind=kCustom, calls=%fused_computation.36 | custom fusion | bytes 32772 | tf_op jit(solution)/shard_map/scatter | solution.py:31
  202.0 0.1 and_select_fusion.1
  202.1 0.1 compare_select_fusion.1
  202.2 0.6 gather_fusion
  202.8 0.2 convert_reduce_fusion.2
  203.0 24.5 %all-to-all-done = bf16[64,2,4096]{2,1,0:T(2,128)(2,1)S(1)} async-done(((bf16[64,2,4096]{2,1,0:T(2,128)(2,1)}), bf16[64,2,4096]{2,1,0:T(2,128)(2,1)S(1)}, u32[]{:S(2)}, u32[]{:S(2)}) %all-to-all-start) | async-done | bytes 1048608 | tf_op jit(solution)/shard_map/all_to_all | solution.py:26
  227.5 0.4 all_to_all.10
  227.9 0.5 convolution_convert_fusion
  228.4 1.3 reshape.37
  (6 shorter events, 0.1 us)
Async XLA Ops:
  6.5 141.4 %copy-start.2 = (f32[4096]{0:T(1024)S(1)}, f32[4096]{0:T(1024)}, u32[]{:S(2)}) copy-start(f32[4096]{0:T(1024)} %param.5) | copy-start | bytes 49156
  6.5 135.3 %all-gather.2.cloned.1.call-start = ((), (), s32[]{:S(2)}) async-start(), calls=%async_computation.1 | async-start | bytes 9437184 | tf_op jit(solution)/shard_map/all_gather | solution.py:48
  141.8 6.1 %copy-start = (bf16[1024,4096]{1,0:T(8,128)(2,1)S(1)}, bf16[1024,4096]{1,0:T(8,128)(2,1)}, u32[]{:S(2)}) copy-start(bf16[1024,4096]{1,0:T(8,128)(2,1)} %all-gather.2.cloned.1.call-done) | copy-start | bytes 25165828
  154.8 16.7 %copy-start.1 = (s32[8192]{0:T(1024)S(1)}, s32[8192]{0:T(1024)}, u32[]{:S(2)}) copy-start(s32[8192]{0:T(1024)} %param.7) | copy-start | bytes 98308
  157.3 70.2 %all-to-all-start = ((bf16[64,2,4096]{2,1,0:T(2,128)(2,1)}), bf16[64,2,4096]{2,1,0:T(2,128)(2,1)S(1)}, u32[]{:S(2)}, u32[]{:S(2)}) async-start(bf16[64,2,4096]{2,1,0:T(2,128)(2,1)} %all_to_all.8), calls=%async_computation | async-start | bytes 2097152 | tf_op jit(solution)/shard_map/all_to_all | solution.py:26
Sparse Core Ops, SparseCore 0:
  10.4 131.3 all-gather.1
where the time goes:
time: 237 us
  waiting for transfers between devices  158 us (67%)
  local copies, waits for them, and re-layouts  34.9 us (15%)
  starting transfers between devices  14.2 us (6%)
  between operations  13.5 us (6%)
  other arithmetic  8.2 us (3%)
  matrix products  7.75 us (3%)
    all_gather x1, waiting for transfers between devices, project(): whole_rows = lax.all_gather(memory_rows, 'tp', axis=1, tiled=True)  133 us
    scatter x1, local copies, waits for them, and re-layouts, to_owners(): inverse = jnp.zeros((block_total,), jnp.int32).at[owner_table].set(jnp.ar...  30.5 us
    all_to_all x1, waiting for transfers between devices, to_owners(): lax.all_to_all(outgoing, 'grp', split_axis=0, concat_axis=0, tiled=True)  24.5 us
    all_to_all x1, starting transfers between devices, to_owners(): lax.all_to_all(outgoing, 'grp', split_axis=0, concat_axis=0, tiled=True)  14.2 us
    dot_general x1, matrix products, project(): keys = jnp.dot(normed, key_weight, preferred_element_type=jnp.float32)  6.84 us
    reduce_sum x1, other arithmetic, project(): row_mean = jnp.sum(values, axis=1, keepdims=True) / width  6.09 us
  transfers between devices with their start and end apart: 2, of which 2 were waited for; matrix products, arithmetic and copies ran while one was open for 14% of the time, Pallas kernels for 0%

commit v1 on v0

--- a/solution.py
+++ b/solution.py
@@ -45,7 +45,13 @@
 
 def project(memory_rows, norm_gain, key_weight):
     width = norm_gain.shape[0]
-    whole_rows = lax.all_gather(memory_rows, "tp", axis=1, tiled=True)
+    scan_terms_now = lambda mat: jnp.concatenate(
+        lax.all_to_all(
+            jnp.stack(lax.axis_size("tp") * [mat]), split_axis=0, concat_axis=0, axis_name="tp"
+        ),
+        axis=1,
+    )
+    whole_rows = scan_terms_now(memory_rows)
     values = whole_rows.astype(jnp.float32)
     row_mean = jnp.sum(values, axis=1, keepdims=True) / width
     row_var = jnp.sum(values * values, axis=1, keepdims=True) / width - row_mean * row_mean

time: 237 us -> 200 us (0.84)
  the two profiles are of different devices: /device:TPU:2 before, /device:TPU:6 now
where the time goes in v1:
time: 200 us
  waiting for transfers between devices  117 us (58%)
  local copies, waits for them, and re-layouts  40.7 us (20%)
  starting transfers between devices  24.7 us (12%)
  other arithmetic  11.8 us (6%)
  matrix products  5.42 us (3%)
    all_to_all x1, waiting for transfers between devices, project(): lax.all_to_all(jnp.stack(lax.axis_size('tp') * [mat]), split_axis=0, conc...  92.6 us
    scatter x1, local copies, waits for them, and re-layouts, to_owners(): inverse = jnp.zeros((block_total,), jnp.int32).at[owner_table].set(jnp.ar...  30.5 us
    all_to_all x1, waiting for transfers between devices, to_owners(): lax.all_to_all(outgoing, 'grp', split_axis=0, concat_axis=0, tiled=True)  24.5 us
    all_to_all x1, starting transfers between devices, to_owners(): lax.all_to_all(outgoing, 'grp', split_axis=0, concat_axis=0, tiled=True)  17.1 us
    all_to_all x1, starting transfers between devices, project(): lax.all_to_all(jnp.stack(lax.axis_size('tp') * [mat]), split_axis=0, conc...  7.57 us
    reduce_sum x1, other arithmetic, project(): row_mean = jnp.sum(values, axis=1, keepdims=True) / width  5.6 us
    convert_element_type x1, other arithmetic, project(): ((values - row_mean) * lax.rsqrt(row_var + EPS) * norm_gain[None, :]).ast...  5.51 us
    dot_general x1, matrix products, project(): keys = jnp.dot(normed, key_weight, preferred_element_type=jnp.float32)  4.52 us
  transfers between devices with their start and end apart: 2, of which 2 were waited for; matrix products, arithmetic and copies ran while one was open for 16% of the time, Pallas kernels for 0%

profile of v1, /device:TPU:6, one launch (start us, length us, event | category | flops | bytes accessed | tf_op | source)
XLA Modules:
  0.0 199.9 jit_solution(9420855359398352423)
XLA Ops:
  0.0 1.5 copy.6
  1.5 4.3 %stack.2 = bf16[8,1024,512]{1,2,0:T(8,128)(2,1)} broadcast(bf16[1024,512]{0,1:T(8,128)(2,1)S(1)} %copy.6), dimensions={1,2} | broadcast | bytes 9437184 | tf_op jit(solution)/shard_map/stack | solution.py:50
  5.8 0.0 copy-start
  5.8 7.6 %all-to-all-start = ((bf16[8,1024,512]{1,2,0:T(8,128)(2,1)}), bf16[8,1024,512]{1,2,0:T(8,128)(2,1)}, u32[]{:S(2)}, u32[]{:S(2)}) async-start(bf16[8,1024,512]{1,2,0:T(8,128)(2,1)} %stack.2), calls=%async_computation | async-start | bytes 16777216 | tf_op jit(solution)/shard_map/all_to_all | solution.py:49
  13.4 0.0 copy-start.1
  13.4 0.0 copy-done
  13.4 0.1 and_select_fusion
  13.4 0.2 convert_reduce_fusion.1
  13.6 0.1 multiply_add_fusion
  13.7 92.6 %all-to-all-done = bf16[8,1024,512]{1,2,0:T(8,128)(2,1)} async-done(((bf16[8,1024,512]{1,2,0:T(8,128)(2,1)}), bf16[8,1024,512]{1,2,0:T(8,128)(2,1)}, u32[]{:S(2)}, u32[]{:S(2)}) %all-to-all-start) | async-done | bytes 8388640 | tf_op jit(solution)/shard_map/all_to_all | solution.py:49
  106.3 5.6 %convert_reduce_fusion = (f32[1024]{0:T(1024)S(1)}, f32[1024]{0:T(1024)S(1)}) fusion(bf16[8,1024,512]{1,2,0:T(8,128)(2,1)} %all-to-all-done), kind=kLoop, calls=%fused_computation.7 | loop fusion | flops 16775168 | bytes 8396800 | tf_op jit(solution)/shard_map/reduce_sum | solution.py:56
  112.0 0.0 copy-done.1
  112.0 0.0 copy-start.2
  112.0 5.5 %fusion.2 = bf16[1024,4096]{0,1:T(8,128)(2,1)S(1)} fusion(bf16[8,1024,512]{1,2,0:T(8,128)(2,1)} %all-to-all-done, f32[4096]{0:T(1024)S(1)} %copy-done.1, f32[1024]{0:T(1024)S(1)} %get-tuple-element.12, f32[1024]{0:T(1024)S(1)} %get-tuple-element.11), kind=kLoop, calls=%fused_computation.5 | loop fusion | flops 20971520 | bytes 16801792 | tf_op jit(solution)/shard_map/convert_element_type | solution.py:58
  117.5 0.0 copy-done.2
  117.5 4.5 %convolution_convert_fusion.2 = bf16[1024,512]{1,0:T(8,128)(2,1)S(1)} fusion(bf16[1024,4096]{0,1:T(8,128)(2,1)S(1)} %fusion.2, bf16[4096,512]{1,0:T(8,128)(2,1)S(1)} %copy-done.2), kind=kOutput, calls=%fused_computation.10 | convolution fusion | flops 4295491584 | bytes 13631488 | tf_op jit(solution)/shard_map/dot_general | solution.py:61
  122.0 0.5 reshape.42
  122.6 0.4 convolution_convert_fusion.1
  123.0 1.5 all_to_all.12
  124.5 17.1 %all-to-all-start.1 = ((bf16[64,2,4096]{2,1,0:T(2,128)(2,1)}), bf16[64,2,4096]{2,1,0:T(2,128)(2,1)S(1)}, u32[]{:S(2)}, u32[]{:S(2)}) async-start(bf16[64,2,4096]{2,1,0:T(2,128)(2,1)} %all_to_all.12), calls=%async_computation.1 | async-start | bytes 2097152 | tf_op jit(solution)/shard_map/all_to_all | solution.py:26
  141.6 30.5 %scatter_custom_fusion = s32[8192]{0:T(1024)S(1)} fusion(s32[8192]{0:T(1024)S(1)} %compare_select_fusion, s32[8192]{0:T(1024)S(1)} %iota.11, s32[]{:T(128)} %constant.54.clone.1), kind=kCustom, calls=%fused_computation.31 | custom fusion | bytes 32772 | tf_op jit(solution)/shard_map/scatter | solution.py:31
  172.1 0.1 and_select_fusion.1
  172.2 0.1 compare_select_fusion.1
  172.3 0.6 gather_fusion
  173.0 0.2 convert_reduce_fusion.2
  173.2 24.5 %all-to-all-done.1 = bf16[64,2,4096]{2,1,0:T(2,128)(2,1)S(1)} async-done(((bf16[64,2,4096]{2,1,0:T(2,128)(2,1)}), bf16[64,2,4096]{2,1,0:T(2,128)(2,1)S(1)}, u32[]{:S(2)}, u32[]{:S(2)}) %all-to-all-start.1) | async-done | bytes 1048608 | tf_op jit(solution)/shard_map/all_to_all | solution.py:26
  197.7 0.4 all_to_all.14
  198.1 0.5 convolution_convert_fusion
  198.6 1.3 reshape.43
  (6 shorter events, 0.1 us)
Async XLA Ops:
  5.8 7.6 %copy-start = (s32[8192]{0:T(1024)S(1)}, s32[8192]{0:T(1024)}, u32[]{:S(2)}) copy-start(s32[8192]{0:T(1024)} %param.7) | copy-start | bytes 98308
  5.8 100.6 %all-to-all-start = ((bf16[8,1024,512]{1,2,0:T(8,128)(2,1)}), bf16[8,1024,512]{1,2,0:T(8,128)(2,1)}, u32[]{:S(2)}, u32[]{:S(2)}) async-start(bf16[8,1024,512]{1,2,0:T(8,128)(2,1)} %stack.2), calls=%async_computation | async-start | bytes 16777216 | tf_op jit(solution)/shard_map/all_to_all | solution.py:49
  13.4 98.6 %copy-start.1 = (f32[4096]{0:T(1024)S(1)}, f32[4096]{0:T(1024)}, u32[]{:S(2)}) copy-start(f32[4096]{0:T(1024)} %param.5) | copy-start | bytes 49156
  112.0 5.5 %copy-start.2 = (bf16[4096,512]{1,0:T(8,128)(2,1)S(1)}, bf16[4096,512]{1,0:T(8,128)(2,1)}, u32[]{:S(2)}) copy-start(bf16[4096,512]{1,0:T(8,128)(2,1)} %param.6) | copy-start | bytes 12582916
  124.5 73.2 %all-to-all-start.1 = ((bf16[64,2,4096]{2,1,0:T(2,128)(2,1)}), bf16[64,2,4096]{2,1,0:T(2,128)(2,1)S(1)}, u32[]{:S(2)}, u32[]{:S(2)}) async-start(bf16[64,2,4096]{2,1,0:T(2,128)(2,1)} %all_to_all.12), calls=%async_computation.1 | async-start | bytes 2097152 | tf_op jit(solution)/shard_map/all_to_all | solution.py:26
